TPU v7x, 32 devices: a whole 2x2x4 slice. The times are simulated.
32 devices in a mesh: grp: 2 (over y), gz: 4 (over z), gx: 2 (over x), row: 2 (over core).
Axes of the slice: x: 2, y: 2, z: 4, core: 2. Of those that a mesh axis runs over, the one named last changes fastest.
Arguments:
- volume: float32 [32, 512, 512], P(('grp', 'gz'), 'gx', 'row'), parts along dimension 0, may hold values from -6 to 6
- tile_table: bfloat16 [64, 128, 128], replicated, may hold values from -0.09375 to 0.09375
- tile_ids: int32 [4, 2, 2, 4, 32], P('gz', 'gx', 'row'), may hold values from 0 to 63
- block_ids: int32 [4, 2, 2, 4, 768], P('gz', 'gx', 'row'), may hold values from 0 to 2047
- live_slots: int32 [4, 2, 2, 4], P('gz', 'gx', 'row'), may hold values from 4 to 32, as said below
- measured: float32 [8, 512, 16], P(('grp', 'gz'), ('gx', 'row')), parts along dimension 0, may hold values from -12 to 12
- row_norm: float32 [4, 512, 16], P('gz', ('gx', 'row')), may hold values from 0.2 to 1
- col_norm: float32 [16, 512, 512], P('gz', 'gx', 'row'), may hold values from 0.5 to 2
Outputs:
- new_volume: float32 [32, 512, 512], P(('grp', 'gz'), 'gx', 'row'), parts along dimension 0
There are 2 independent parts, one for each index of `grp`. A program takes and returns all parts, laid end to end along the dimension named above; an argument that names none is the same for every part. Nothing has to cross between parts.
Inputs may be any that keep to these rules, and one draw needn't show every extreme that they name: `block_ids`: indices of voxel blocks of the piece itself. `live_slots`: 32 is reached by some angle of some piece in every draw.
All inputs are finite; a program needn't handle non-finite values.
Results may differ from a plain program's by a relative error of at most 0.004.
Values may be sent and summed in bfloat16 or wider, within the bound.
A program may use at most 64 MiB of HBM per device.

v0:
```python
import math
import jax
import jax.numpy as jnp
from jax import lax
from jax.sharding import PartitionSpec as P


def extended_2(cells, sides, width):
    for axis, dim in sides:
        count = lax.axis_size(axis)
        ends = count - 1
        head = lax.slice_in_dim(cells, 0, width, axis=dim)
        tail = lax.slice_in_dim(cells, cells.shape[dim] - width, cells.shape[dim], axis=dim)
        cells = jnp.concatenate(
            [
                lax.ppermute(tail, axis, [(i, (i + 1) % count) for i in range(ends)]),
                cells,
                lax.ppermute(head, axis, [((i + 1) % count, i) for i in range(ends)]),
            ],
            axis=dim,
        )
    return cells


def slot_loop(slot_step, initial, tile_rows, block_rows, live_rows):
    slot_count = tile_rows.shape[1]
    position = jnp.arange(slot_count, dtype=jnp.int32)
    in_use = position[None, :] < live_rows[:, None]
    return slot_step(initial, tile_rows, block_rows, in_use)


def to_windows(row_data, slab_count, slab_depth):
    angles, columns, total_rows = row_data.shape
    padded = jnp.pad(row_data, ((0, 0), (0, 0), (1, 1)))
    head_rows = padded[:, :, :total_rows].reshape(angles, columns, slab_count, slab_depth)
    tail_rows = padded[:, :, 2:].reshape(angles, columns, slab_count, slab_depth)[
        :, :, :, slab_depth - 2 :
    ]
    joined = jnp.concatenate([head_rows, tail_rows], axis=3)
    return joined.transpose(0, 2, 1, 3)


def on_device(volume, tile_table, tile_ids, block_ids, live_slots, measured, row_norm, col_norm):
    slab_depth, column_width, half_width = volume.shape
    tile_count, tile_size = (tile_table.shape[0], tile_table.shape[1])
    angle_count = tile_ids.shape[3]
    slot_count = tile_ids.shape[4]
    window = slab_depth + 2
    block_cols = block_ids.shape[4] // (slot_count * window)
    det_width = block_cols * tile_size
    block_count = slab_depth * column_width * half_width // tile_size
    voxel_rows = volume.astype(jnp.bfloat16).reshape(block_count, tile_size)
    angle_block = math.gcd(angle_count, 2)
    step_count = angle_count // angle_block
    tile_steps = tile_ids.reshape(step_count, angle_block, slot_count)
    block_steps = block_ids.reshape(step_count, angle_block, slot_count, window, block_cols)
    live_steps = live_slots.reshape(step_count, angle_block)
    tile_numbers = jnp.arange(tile_count, dtype=jnp.int32)
    block_numbers = jnp.arange(block_count, dtype=jnp.int32)

    def pick_tiles(tile_part):
        tile_hot = (tile_part[:, :, None] == tile_numbers[None, None, :]).astype(jnp.bfloat16)
        picked = jnp.einsum(
            "akt,tdv->akdv", tile_hot, tile_table, preferred_element_type=jnp.float32
        )
        return picked.astype(jnp.bfloat16)

    def block_table(block_part, in_use):
        matches = block_part[:, :, :, :, None] == block_numbers[None, None, None, None, :]
        return (matches & in_use[:, :, None, None, None]).astype(jnp.bfloat16)

    slab_count = lax.axis_size("gz")
    own_angles, local_cols = (measured.shape[0], measured.shape[1])
    measured_win = to_windows(measured, slab_count, slab_depth).reshape(
        own_angles, slab_count, local_cols * window
    )
    norm_win = to_windows(row_norm, slab_count, slab_depth).reshape(
        own_angles, slab_count, local_cols * window
    )
    arrived = (
        lax.all_to_all(measured_win, "gz", split_axis=1, concat_axis=0, tiled=True),
        lax.all_to_all(norm_win, "gz", split_axis=1, concat_axis=0, tiled=True),
    )
    spread_out = (
        lax.all_gather(
            arrived[0].reshape(angle_count, local_cols * window), ("gx", "row"), axis=1, tiled=True
        ),
        lax.all_gather(
            arrived[1].reshape(angle_count, local_cols * window), ("gx", "row"), axis=1, tiled=True
        ),
    )
    target = spread_out[0].reshape(angle_count, det_width, window).transpose(0, 2, 1)
    weights = spread_out[1].reshape(angle_count, det_width, window).transpose(0, 2, 1)
    out_shape = (window, block_cols, tile_size)

    def project_angle_step(unused, inputs):
        tile_rows, block_rows, live_rows = inputs

        def slot_step(running, tile_part, block_part, in_use):
            picked = pick_tiles(tile_part)
            block_hot = block_table(block_part, in_use)
            voxels = jnp.einsum(
                "akwqn,nv->akwqv", block_hot, voxel_rows, preferred_element_type=jnp.float32
            )
            voxels = voxels.astype(jnp.bfloat16)
            return jnp.einsum(
                "akdv,akwqv->awqd", picked, voxels, preferred_element_type=jnp.float32
            )

        initial = jnp.zeros((angle_block,) + out_shape, jnp.float32)
        return (unused, slot_loop(slot_step, initial, tile_rows, block_rows, live_rows))

    ignored, stacked = lax.scan(
        project_angle_step, jnp.int32(0), (tile_steps, block_steps, live_steps)
    )
    partial_value = stacked.reshape((angle_count,) + out_shape).reshape(
        angle_count, window, det_width
    )
    total_proj = lax.psum(partial_value, ("gx", "row"))
    extended = extended_2(total_proj, (("gz", 1),), 2)
    folded = (
        total_proj.at[:, :2].add(extended[:, :2]).at[:, window - 2 :].add(extended[:, window + 2 :])
    )
    residual = (weights * (target - folded)).astype(jnp.bfloat16)
    res_steps = residual.reshape(step_count, angle_block, window, block_cols, tile_size)

    def back_angle_step(running_sum, inputs):
        tile_rows, block_rows, live_rows, res_rows = inputs

        def slot_step(running, tile_part, block_part, in_use):
            picked = pick_tiles(tile_part)
            block_hot = block_table(block_part, in_use)
            spread = jnp.einsum(
                "akdv,awqd->akwqv", picked, res_rows, preferred_element_type=jnp.float32
            )
            upper_part = spread.astype(jnp.bfloat16)
            lower_part = (spread - upper_part.astype(jnp.float32)).astype(jnp.bfloat16)
            added = jnp.einsum(
                "akwqn,akwqv->nv", block_hot, upper_part, preferred_element_type=jnp.float32
            )
            added = added + jnp.einsum(
                "akwqn,akwqv->nv", block_hot, lower_part, preferred_element_type=jnp.float32
            )
            return running + added

        return (slot_loop(slot_step, running_sum, tile_rows, block_rows, live_rows), None)

    initial = jnp.zeros((block_count, tile_size), jnp.float32)
    result, ignored = lax.scan(
        back_angle_step, initial, (tile_steps, block_steps, live_steps, res_steps)
    )
    return volume + col_norm * result.reshape(slab_depth, column_width, half_width)


def solution(mesh):
    placed = (
        P(("grp", "gz"), "gx", "row"),
        P(),
        P("gz", "gx", "row", None, None),
        P("gz", "gx", "row", None, None),
        P("gz", "gx", "row", None),
        P(("grp", "gz"), ("gx", "row"), None),
        P("gz", ("gx", "row"), None),
        P("gz", "gx", "row"),
    )
    return jax.shard_map(
        on_device,
        mesh=mesh,
        in_specs=placed,
        out_specs=P(("grp", "gz"), "gx", "row"),
        check_vma=False,
    )
```

profile of v0, /device:TPU:0, one launch (start us, length us, event | category | flops | bytes accessed | tf_op | source)
XLA Modules:
  0.0 91.1 jit_solution(14383756225101299012)
XLA Ops:
  0.0 0.0 copy-start.3
  0.0 0.0 copy-start.6
  0.0 3.0 %copy.90 = bf16[64,128,128]{2,0,1:T(8,128)(2,1)S(1)} copy(bf16[64,128,128]{2,1,0:T(8,128)(2,1)} %param.17) | data formatting | bytes 4194304
  3.0 0.0 copy-done.3
  3.0 0.0 copy-start.2
  3.0 0.2 reshape.178
  3.2 0.2 copy.89
  3.4 0.5 broadcast.83
  3.9 0.0 copy-done.6
  3.9 0.7 reduce.9
  4.6 0.1 reshape.179
  4.7 1.3 %convert_element_type.31 = bf16[4,256,256]{2,1,0:T(8,128)(2,1)S(1)} convert(f32[4,256,256]{2,1,0:T(8,128)} %param.16) | non-fusion elementwise | flops 262144 | bytes 1572864 | tf_op jit(solution)/shard_map/convert_element_type | solution.py:52
  6.0 1.0 %reshape.190 = bf16[2048,128]{1,0:T(8,128)(2,1)} reshape(bf16[4,256,256]{2,1,0:T(8,128)(2,1)S(1)} %convert_element_type.31) | data formatting | bytes 1048576 | tf_op jit(solution)/shard_map/reshape | solution.py:52
  6.9 0.0 copy-done.2
  6.9 0.0 copy-start.4
  6.9 0.0 copy-start.5
  7.0 12.0 %while.24 = (s32[]{:T(128)}, f32[2,2,6,4,128]{4,3,1,0,2:T(4,128)S(1)}, s32[2,2,32,6,4]{2,4,3,1,0:T(4,128)S(1)}, s32[2,2]{1,0:T(2,128)S(1)}, bf16[2048,128]{1,0:T...) while((s32[]{:T(128)}, ...), condition=%wide.region_1.2_spmd.clone, body=%wide.region_0.1_spmd.clone.sunk | while | flops 997396544 | bytes 7703549 | solution.py:113
  7.0 0.1 iota_compare_fusion.8
  7.0 3.8 %fusion.102 = bf16[2,32,6,4,128]{4,1,3,2,0:T(8,128)(2,1)S(1)} fusion(s32[2,32,6,4]{1,3,2,0:T(4,128)S(1)} %dynamic-slice_bitcast_fusion.6, pred[2,32]{1,0:T(4,128)(4,1)S(1)} %iota_compare_fusion.8, bf16[2048,128]{1,0:T(8,128)(2,1)} %get-tuple-element.373), kind=kOutput, calls=%fused_computation.14.clone.1 | convolution fusion | flops 811794432 | bytes 923712 | tf_op jit(solution)/shard_map/while/body/eval_jaxpr/akwqn,nv->akwqv/dot_general | solution.py:102
  10.8 0.8 convert_bitcast_fusion.4
  11.6 1.3 %fusion.103 = f32[1,2,6,4,128]{4,2,3,1,0:T(8,128)S(1)} fusion(bf16[2,32,128,128,1]{3,1,2,0,4:T(8,128)(2,1)S(1)} %convert_bitcast_fusion.4, bf16[2,32,6,4,128]{4,1,3,2,0:T(8,128)(2,1)S(1)} %fusion.102), kind=kOutput, calls=%fused_computation.15.clone.1 | convolution fusion | flops 50331648 | bytes 2514944 | tf_op jit(solution)/shard_map/while/body/eval_jaxpr/akdv,akwqv->awqd/dot_general | solution.py:106
  13.0 0.1 iota_compare_fusion.8
  13.1 3.8 %fusion.102 = bf16[2,32,6,4,128]{4,1,3,2,0:T(8,128)(2,1)S(1)} fusion(s32[2,32,6,4]{1,3,2,0:T(4,128)S(1)} %dynamic-slice_bitcast_fusion.6, pred[2,32]{1,0:T(4,128)(4,1)S(1)} %iota_compare_fusion.8, bf16[2048,128]{1,0:T(8,128)(2,1)} %get-tuple-element.373), kind=kOutput, calls=%fused_computation.14.clone.1 | convolution fusion | flops 811794432 | bytes 923712 | tf_op jit(solution)/shard_map/while/body/eval_jaxpr/akwqn,nv->akwqv/dot_general | solution.py:102
  16.9 0.8 convert_bitcast_fusion.4
  17.6 1.3 %fusion.103 = f32[1,2,6,4,128]{4,2,3,1,0:T(8,128)S(1)} fusion(bf16[2,32,128,128,1]{3,1,2,0,4:T(8,128)(2,1)S(1)} %convert_bitcast_fusion.4, bf16[2,32,6,4,128]{4,1,3,2,0:T(8,128)(2,1)S(1)} %fusion.102), kind=kOutput, calls=%fused_computation.15.clone.1 | convolution fusion | flops 50331648 | bytes 2514944 | tf_op jit(solution)/shard_map/while/body/eval_jaxpr/akdv,akwqv->awqd/dot_general | solution.py:106
  19.0 13.2 %psum.7 = f32[4,6,512]{2,0,1:T(4,128)S(1)} all-reduce(f32[4,6,512]{2,0,1:T(4,128)S(1)} %reshape_reshape.3), channel_id=1, replica_groups=mesh['grp'=2,'gz'=4,'gx'=2,'row'=2] {'gx','row'}, use_global_device_ids=true, to_apply=%region_2.3 | all-reduce | flops 12288 | bytes 98304 | tf_op jit(solution)/shard_map/psum | solution.py:119
  32.2 3.5 %collective-permute-start = (f32[4,2,512]{2,0,1:T(4,128)S(1)}, f32[4,2,512]{2,0,1:T(4,128)S(1)}, u32[]{:S(2)}, u32[]{:S(2)}) collective-permute-start(f32[4,2,512]{2,0,1:T(4,128)S(1)} %slice.82), channel_id=1, source_target_pairs={{0,4},{4,8},{8,12},{1,5},{5,9},{9,13},{2,6},{6,10},{10,14},{3,7},{... | collective-permute-start | bytes 49160 | tf_op jit(solution)/shard_map/ppermute | solution.py:16
  35.7 0.0 copy-done.4
  35.8 0.1 copy.81
  36.0 0.8 reshape.209
  36.7 3.9 %all-to-all-start = ((f32[1,4,768]{2,0,1:T(1,128)}), f32[1,4,768]{2,0,1:T(1,128)S(1)}, u32[]{:S(2)}, u32[]{:S(2)}) async-start(f32[1,4,768]{2,0,1:T(1,128)} %reshape.209), calls=%async_computation | async-start | bytes 24576 | tf_op jit(solution)/shard_map/all_to_all | solution.py:82
  40.6 0.0 copy-done.5
  40.7 0.3 copy.92
  40.9 0.2 copy.86
  41.1 0.8 reshape.210
  41.9 0.0 collective-permute-done
  41.9 1.3 %collective-permute-start.1 = (f32[4,2,512]{2,0,1:T(4,128)S(1)}, f32[4,2,512]{2,0,1:T(4,128)S(1)}, u32[]{:S(2)}, u32[]{:S(2)}) collective-permute-start(f32[4,2,512]{2,0,1:T(4,128)S(1)} %get-tuple-element.261), channel_id=1, source_target_pairs={{4,0},{8,4},{12,8},{5,1},{9,5},{13,9},{6,2},{10,6},{14,10},{7,3},{... | collective-permute-start | bytes 49160 | tf_op jit(solution)/shard_map/ppermute | solution.py:18
  43.2 3.0 %all-to-all-done = f32[1,4,768]{2,0,1:T(1,128)S(1)} async-done(((f32[1,4,768]{2,0,1:T(1,128)}), f32[1,4,768]{2,0,1:T(1,128)S(1)}, u32[]{:S(2)}, u32[]{:S(2)}) %all-to-all-start) | async-done | bytes 12320 | tf_op jit(solution)/shard_map/all_to_all | solution.py:82
  46.2 3.3 %all-to-all-start.1 = ((f32[1,4,768]{2,0,1:T(1,128)}), f32[1,4,768]{2,0,1:T(1,128)S(1)}, u32[]{:S(2)}, u32[]{:S(2)}) async-start(f32[1,4,768]{2,0,1:T(1,128)} %reshape.210), calls=%async_computation.1 | async-start | bytes 24576 | tf_op jit(solution)/shard_map/all_to_all | solution.py:81
  49.5 5.2 %all-gather = f32[1,4,3072]{2,0,1:T(1,128)S(1)} all-gather(f32[1,4,768]{2,0,1:T(1,128)S(1)} %all-to-all-done), channel_id=2, replica_groups=mesh['grp'=2,'gz'=4,'gx'=2,'row'=2] {'gx','row'}, dimensions={2}, use_global_device_ids=true | all-gather | bytes 61440 | tf_op jit(solution)/shard_map/all_gather | solution.py:88
  54.7 0.1 reduce.5
  54.8 1.0 %reshape.184 = f32[4,512,6]{2,1,0:T(8,128)S(1)} reshape(f32[4,3072]{1,0:T(4,128)S(1)} %reduce.5) | data formatting | bytes 98304 | tf_op jit(solution)/shard_map/reshape | solution.py:93
  55.9 0.3 copy.83
  56.2 0.0 all-to-all-done.1
  56.2 5.4 %all-gather.1 = f32[1,4,3072]{2,0,1:T(1,128)S(1)} all-gather(f32[1,4,768]{2,0,1:T(1,128)S(1)} %all-to-all-done.1), channel_id=3, replica_groups=mesh['grp'=2,'gz'=4,'gx'=2,'row'=2] {'gx','row'}, dimensions={2}, use_global_device_ids=true | all-gather | bytes 61440 | tf_op jit(solution)/shard_map/all_gather | solution.py:85
  61.6 0.1 reduce.6
  61.7 1.0 %reshape.189 = f32[4,512,6]{2,1,0:T(8,128)S(1)} reshape(f32[4,3072]{1,0:T(4,128)S(1)} %reduce.6) | data formatting | bytes 98304 | tf_op jit(solution)/shard_map/reshape | solution.py:92
  62.8 0.3 copy.88
  63.1 0.0 collective-permute-done.1
  63.2 24.8 %while.25 = (s32[]{:T(128)}, f32[2048,128]{1,0:T(8,128)}, s32[2,2,32,6,4]{2,3,4,1,0:T(8,128)S(1)}, s32[2,2]{1,0:T(2,128)S(1)}, bf16[2,2,6,4,128]{4,3,1,0,2:T(4,1...) while((s32[]{:T(128)}, f32[2048,128]{1,0:T(8,128)}, ...), condition=%wide.region_4.5_spmd.clone, body=%wide.region_3.4_spmd.clone.sunk | while | flops 1810370560 | bytes 12907599 | solution.py:149
  63.2 0.7 convert_bitcast_fusion.5
  64.0 0.7 fusion.113
  64.7 0.1 iota_compare_fusion.9
  64.8 4.7 %fusion.114 = f32[2048,128]{1,0:T(8,128)} fusion(s32[2,32,6,4]{1,2,3,0:T(8,128)S(1)} %dynamic-slice_bitcast_fusion.7, pred[2,32]{1,0:T(4,128)(4,1)S(1)} %iota_compare_fusion.9, f32[2,6,4,32,128]{4,1,3,2,0:T(8,128)S(1)} %fusion.113), kind=kOutput, calls=%fused_computation.36.clone.1 | convolution fusion | flops 811597824 | bytes 1841216 | tf_op jit(solution)/shard_map/while/body/eval_jaxpr/akwqn,akwqv->nv/dot_general | solution.py:138
  69.5 5.9 %fusion.115 = f32[2048,128]{1,0:T(8,128)} fusion(f32[2048,128]{1,0:T(8,128)} %fusion.114, s32[2,32,6,4]{1,2,3,0:T(8,128)S(1)} %dynamic-slice_bitcast_fusion.7, pred[2,32]{1,0:T(4,128)(4,1)S(1)} %iota_compare_fusion.9, f32[2048,128]{1,0:T(8,128)} %get-tuple-element.387, pred[]{:T(512)S(6)} %compare.16, f32[2,6,4,32,128]{4,1,3,2,0:T(8,128)S(1)} %fusion.113), kind=kOutput, calls=%fused_computation.39.clone.1 | convolution fusion | flops 813170688 | bytes 3938369 | tf_op jit(solution)/shard_map/while/body/eval_jaxpr/akwqn,akwqv->nv/dot_general | solution.py:141
  75.5 0.8 convert_bitcast_fusion.5
  76.2 0.7 fusion.113
  77.0 0.1 iota_compare_fusion.9
  77.1 4.7 %fusion.114 = f32[2048,128]{1,0:T(8,128)} fusion(s32[2,32,6,4]{1,2,3,0:T(8,128)S(1)} %dynamic-slice_bitcast_fusion.7, pred[2,32]{1,0:T(4,128)(4,1)S(1)} %iota_compare_fusion.9, f32[2,6,4,32,128]{4,1,3,2,0:T(8,128)S(1)} %fusion.113), kind=kOutput, calls=%fused_computation.36.clone.1 | convolution fusion | flops 811597824 | bytes 1841216 | tf_op jit(solution)/shard_map/while/body/eval_jaxpr/akwqn,akwqv->nv/dot_general | solution.py:138
  81.8 6.2 %fusion.115 = f32[2048,128]{1,0:T(8,128)} fusion(f32[2048,128]{1,0:T(8,128)} %fusion.114, s32[2,32,6,4]{1,2,3,0:T(8,128)S(1)} %dynamic-slice_bitcast_fusion.7, pred[2,32]{1,0:T(4,128)(4,1)S(1)} %iota_compare_fusion.9, f32[2048,128]{1,0:T(8,128)} %get-tuple-element.387, pred[]{:T(512)S(6)} %compare.16, f32[2,6,4,32,128]{4,1,3,2,0:T(8,128)S(1)} %fusion.113), kind=kOutput, calls=%fused_computation.39.clone.1 | convolution fusion | flops 813170688 | bytes 3938369 | tf_op jit(solution)/shard_map/while/body/eval_jaxpr/akwqn,akwqv->nv/dot_general | solution.py:141
  88.0 1.7 %reshape.193 = f32[4,256,256]{2,1,0:T(8,128)S(1)} reshape(f32[2048,128]{1,0:T(8,128)} %get-tuple-element.124) | data formatting | bytes 2097152 | tf_op jit(solution)/shard_map/reshape | solution.py:152
  89.7 0.0 copy-done
  89.7 0.2 copy-done.1
  89.9 1.2 %multiply_add_fusion = f32[4,256,256]{2,1,0:T(8,128)} fusion(f32[4,256,256]{2,1,0:T(8,128)S(1)} %copy-done, f32[4,256,256]{2,1,0:T(8,128)S(1)} %copy-done.1, f32[4,256,256]{2,1,0:T(8,128)S(1)} %reshape.193), kind=kLoop, calls=%fused_computation.60 | loop fusion | flops 524288 | bytes 4194304 | tf_op jit(solution)/shard_map/add | solution.py:152
  (36 shorter events, 0.3 us)
Async XLA Ops:
  0.0 3.0 %copy-start.3 = (s32[1,1,1,4,768]{4,3,2,1,0:T(4,128)S(1)}, s32[1,1,1,4,768]{4,3,2,1,0:T(4,128)}, u32[]{:S(2)}) copy-start(s32[1,1,1,4,768]{4,3,2,1,0:T(4,128)} %param.19) | copy-start | bytes 36868
  0.0 3.9 %copy-start.6 = (s32[1,1,1,4]{3,2,1,0:T(1,128)S(1)}, s32[1,1,1,4]{3,2,1,0:T(1,128)}, u32[]{:S(2)}) copy-start(s32[1,1,1,4]{3,2,1,0:T(1,128)} %param.20) | copy-start | bytes 52
  3.0 4.0 %copy-start.2 = (s32[1,1,1,4,32]{4,3,2,1,0:T(4,128)S(1)}, s32[1,1,1,4,32]{4,3,2,1,0:T(4,128)}, u32[]{:S(2)}) copy-start(s32[1,1,1,4,32]{4,3,2,1,0:T(4,128)} %param.18) | copy-start | bytes 1540
  6.9 28.8 %copy-start.4 = (f32[1,128,16]{1,2,0:T(8,128)S(1)}, f32[1,128,16]{1,2,0:T(8,128)}, u32[]{:S(2)}) copy-start(f32[1,128,16]{1,2,0:T(8,128)} %param.22) | copy-start | bytes 24580
  6.9 33.7 %copy-start.5 = (f32[1,128,16]{1,2,0:T(8,128)S(1)}, f32[1,128,16]{1,2,0:T(8,128)}, u32[]{:S(2)}) copy-start(f32[1,128,16]{1,2,0:T(8,128)} %param.21) | copy-start | bytes 24580
  32.2 9.7 %collective-permute-start = (f32[4,2,512]{2,0,1:T(4,128)S(1)}, f32[4,2,512]{2,0,1:T(4,128)S(1)}, u32[]{:S(2)}, u32[]{:S(2)}) collective-permute-start(f32[4,2,512]{2,0,1:T(4,128)S(1)} %slice.82), channel_id=1, source_target_pairs={{0,4},{4,8},{8,12},{1,5},{5,9},{9,13},{2,6},{6,10},{10,14},{3,7},{... | collective-permute-start | bytes 49160 | tf_op jit(solution)/shard_map/ppermute | solution.py:16
  36.7 9.5 %all-to-all-start = ((f32[1,4,768]{2,0,1:T(1,128)}), f32[1,4,768]{2,0,1:T(1,128)S(1)}, u32[]{:S(2)}, u32[]{:S(2)}) async-start(f32[1,4,768]{2,0,1:T(1,128)} %reshape.209), calls=%async_computation | async-start | bytes 24576 | tf_op jit(solution)/shard_map/all_to_all | solution.py:82
  41.9 21.2 %collective-permute-start.1 = (f32[4,2,512]{2,0,1:T(4,128)S(1)}, f32[4,2,512]{2,0,1:T(4,128)S(1)}, u32[]{:S(2)}, u32[]{:S(2)}) collective-permute-start(f32[4,2,512]{2,0,1:T(4,128)S(1)} %get-tuple-element.261), channel_id=1, source_target_pairs={{4,0},{8,4},{12,8},{5,1},{9,5},{13,9},{6,2},{10,6},{14,10},{7,3},{... | collective-permute-start | bytes 49160 | tf_op jit(solution)/shard_map/ppermute | solution.py:18
  46.2 10.0 %all-to-all-start.1 = ((f32[1,4,768]{2,0,1:T(1,128)}), f32[1,4,768]{2,0,1:T(1,128)S(1)}, u32[]{:S(2)}, u32[]{:S(2)}) async-start(f32[1,4,768]{2,0,1:T(1,128)} %reshape.210), calls=%async_computation.1 | async-start | bytes 24576 | tf_op jit(solution)/shard_map/all_to_all | solution.py:81
  88.0 1.7 %copy-start = (f32[4,256,256]{2,1,0:T(8,128)S(1)}, f32[4,256,256]{2,1,0:T(8,128)}, u32[]{:S(2)}) copy-start(f32[4,256,256]{2,1,0:T(8,128)} %param.16) | copy-start | bytes 3145732
  88.0 1.9 %copy-start.1 = (f32[4,256,256]{2,1,0:T(8,128)S(1)}, f32[4,256,256]{2,1,0:T(8,128)}, u32[]{:S(2)}) copy-start(f32[4,256,256]{2,1,0:T(8,128)} %param.23) | copy-start | bytes 3145732
where the time goes:
time: 91.6 us; the launch traced here: 91.1 us
  matrix products  36.2 us (40%)
  blocking collectives  23.8 us (26%)
  local copies, waits for them, and re-layouts  12 us (13%)
  starting transfers between devices  11.9 us (13%)
  other arithmetic  3.73 us (4%)
  waiting for transfers between devices  3.01 us (3%)
    psum x1, blocking collectives, on_device(): total_proj = lax.psum(partial_value, ('gx', 'row'))  13.2 us
    dot_general x2, matrix products, slot_step(): jnp.einsum('akwqn,akwqv->nv', block_hot, lower_part, preferred_element_ty...  12.2 us
    dot_general x2, matrix products, slot_step(): jnp.einsum('akwqn,akwqv->nv', block_hot, upper_part, preferred_element_ty...  9.4 us
    dot_general x2, matrix products, slot_step(): jnp.einsum('akwqn,nv->akwqv', block_hot, voxel_rows, preferred_element_ty...  7.55 us
    all_gather x1, blocking collectives, on_device(): lax.all_gather(arrived[0].reshape(angle_count, local_cols * window), ('gx...  5.38 us
    all_gather x1, blocking collectives, on_device(): lax.all_gather(arrived[1].reshape(angle_count, local_cols * window), ('gx...  5.19 us
    unnamed x18, local copies, waits for them, and re-layouts  4.17 us
    all_to_all x1, starting transfers between devices, on_device(): lax.all_to_all(norm_win, 'gz', split_axis=1, concat_axis=0, tiled=True)  3.86 us
  transfers between devices with their start and end apart: 4, of which 1 were waited for; matrix products, arithmetic and copies ran while one was open for 6% of the time, Pallas kernels for 0%

commit v1 on v0

--- a/solution.py
+++ b/solution.py
@@ -116,7 +116,8 @@
     partial_value = stacked.reshape((angle_count,) + out_shape).reshape(
         angle_count, window, det_width
     )
-    total_proj = lax.psum(partial_value, ("gx", "row"))
+    blocks = lax.all_gather(partial_value, ("gx", "row"))
+    total_proj = jnp.sum(blocks, axis=0)
     extended = extended_2(total_proj, (("gz", 1),), 2)
     folded = (
         total_proj.at[:, :2].add(extended[:, :2]).at[:, window - 2 :].add(extended[:, window + 2 :])

time: 91.6 us -> 85.4 us (0.932)
  blocking collectives: 23.8 us -> 17.4 us
    psum x1 -> x0, blocking collectives: 13.2 us -> none  [on_device(): total_proj = lax.psum(partial_value, ('gx', 'row'))]
    all_gather x0 -> x1, blocking collectives: none -> 6.86 us  [on_device(): blocks = lax.all_gather(partial_value, ('gx', 'row'))]
where the time goes in v1:
time: 85.4 us; the launch traced here: 84.9 us
  matrix products  36.2 us (42%)
  blocking collectives  17.4 us (20%)
  starting transfers between devices  12.1 us (14%)
  local copies, waits for them, and re-layouts  12 us (14%)
  other arithmetic  3.77 us (4%)
  waiting for transfers between devices  3.01 us (4%)
    dot_general x2, matrix products, slot_step(): jnp.einsum('akwqn,akwqv->nv', block_hot, lower_part, preferred_element_ty...  12.2 us
    dot_general x2, matrix products, slot_step(): jnp.einsum('akwqn,akwqv->nv', block_hot, upper_part, preferred_element_ty...  9.4 us
    dot_general x2, matrix products, slot_step(): jnp.einsum('akwqn,nv->akwqv', block_hot, voxel_rows, preferred_element_ty...  7.55 us
    all_gather x1, blocking collectives, on_device(): blocks = lax.all_gather(partial_value, ('gx', 'row'))  6.86 us
    all_gather x1, blocking collectives, on_device(): lax.all_gather(arrived[0].reshape(angle_count, local_cols * window), ('gx...  5.38 us
    all_gather x1, blocking collectives, on_device(): lax.all_gather(arrived[1].reshape(angle_count, local_cols * window), ('gx...  5.19 us
    unnamed x18, local copies, waits for them, and re-layouts  4.17 us
    all_to_all x1, starting transfers between devices, on_device(): lax.all_to_all(norm_win, 'gz', split_axis=1, concat_axis=0, tiled=True)  3.85 us
  transfers between devices with their start and end apart: 4, of which 1 were waited for; matrix products, arithmetic and copies ran while one was open for 6% of the time, Pallas kernels for 0%

profile of v1, /device:TPU:0, one launch (start us, length us, event | category | flops | bytes accessed | tf_op | source)
XLA Modules:
  0.0 84.9 jit_solution(381643714209089378)
XLA Ops:
  0.0 0.0 copy-start.3
  0.0 0.0 copy-start.6
  0.0 3.0 %copy.107 = bf16[64,128,128]{2,0,1:T(8,128)(2,1)S(1)} copy(bf16[64,128,128]{2,1,0:T(8,128)(2,1)} %param.17) | data formatting | bytes 4194304
  3.0 0.0 copy-done.3
  3.0 0.0 copy-start.2
  3.0 0.2 reshape.178
  3.2 0.2 copy.106
  3.4 0.5 broadcast.83
  3.9 0.0 copy-done.6
  3.9 0.7 reduce.9
  4.6 0.1 reshape.179
  4.7 1.3 %convert_element_type.31 = bf16[4,256,256]{2,1,0:T(8,128)(2,1)S(1)} convert(f32[4,256,256]{2,1,0:T(8,128)} %param.16) | non-fusion elementwise | flops 262144 | bytes 1572864 | tf_op jit(solution)/shard_map/convert_element_type | solution.py:52
  6.0 1.0 %reshape.190 = bf16[2048,128]{1,0:T(8,128)(2,1)} reshape(bf16[4,256,256]{2,1,0:T(8,128)(2,1)S(1)} %convert_element_type.31) | data formatting | bytes 1048576 | tf_op jit(solution)/shard_map/reshape | solution.py:52
  6.9 0.0 copy-done.2
  6.9 0.0 copy-start.4
  6.9 0.0 copy-start.5
  7.0 12.0 %while.24 = (s32[]{:T(128)}, f32[2,2,6,4,128]{4,3,1,0,2:T(4,128)S(1)}, s32[2,2,32,6,4]{2,4,3,1,0:T(4,128)S(1)}, s32[2,2]{1,0:T(2,128)S(1)}, bf16[2048,128]{1,0:T...) while((s32[]{:T(128)}, ...), condition=%wide.region_1.2_spmd.clone, body=%wide.region_0.1_spmd.clone.sunk | while | flops 997396544 | bytes 7703549 | solution.py:113
  7.0 0.1 iota_compare_fusion.8
  7.0 3.8 %fusion.102 = bf16[2,32,6,4,128]{4,1,3,2,0:T(8,128)(2,1)S(1)} fusion(s32[2,32,6,4]{1,3,2,0:T(4,128)S(1)} %dynamic-slice_bitcast_fusion.6, pred[2,32]{1,0:T(4,128)(4,1)S(1)} %iota_compare_fusion.8, bf16[2048,128]{1,0:T(8,128)(2,1)} %get-tuple-element.387), kind=kOutput, calls=%fused_computation.14.clone.1 | convolution fusion | flops 811794432 | bytes 923712 | tf_op jit(solution)/shard_map/while/body/eval_jaxpr/akwqn,nv->akwqv/dot_general | solution.py:102
  10.8 0.8 convert_bitcast_fusion.4
  11.6 1.3 %fusion.103 = f32[1,2,6,4,128]{4,2,3,1,0:T(8,128)S(1)} fusion(bf16[2,32,128,128,1]{3,1,2,0,4:T(8,128)(2,1)S(1)} %convert_bitcast_fusion.4, bf16[2,32,6,4,128]{4,1,3,2,0:T(8,128)(2,1)S(1)} %fusion.102), kind=kOutput, calls=%fused_computation.15.clone.1 | convolution fusion | flops 50331648 | bytes 2514944 | tf_op jit(solution)/shard_map/while/body/eval_jaxpr/akdv,akwqv->awqd/dot_general | solution.py:106
  13.0 0.1 iota_compare_fusion.8
  13.1 3.8 %fusion.102 = bf16[2,32,6,4,128]{4,1,3,2,0:T(8,128)(2,1)S(1)} fusion(s32[2,32,6,4]{1,3,2,0:T(4,128)S(1)} %dynamic-slice_bitcast_fusion.6, pred[2,32]{1,0:T(4,128)(4,1)S(1)} %iota_compare_fusion.8, bf16[2048,128]{1,0:T(8,128)(2,1)} %get-tuple-element.387), kind=kOutput, calls=%fused_computation.14.clone.1 | convolution fusion | flops 811794432 | bytes 923712 | tf_op jit(solution)/shard_map/while/body/eval_jaxpr/akwqn,nv->akwqv/dot_general | solution.py:102
  16.9 0.8 convert_bitcast_fusion.4
  17.6 1.3 %fusion.103 = f32[1,2,6,4,128]{4,2,3,1,0:T(8,128)S(1)} fusion(bf16[2,32,128,128,1]{3,1,2,0,4:T(8,128)(2,1)S(1)} %convert_bitcast_fusion.4, bf16[2,32,6,4,128]{4,1,3,2,0:T(8,128)(2,1)S(1)} %fusion.102), kind=kOutput, calls=%fused_computation.15.clone.1 | convolution fusion | flops 50331648 | bytes 2514944 | tf_op jit(solution)/shard_map/while/body/eval_jaxpr/akdv,akwqv->awqd/dot_general | solution.py:106
  19.0 6.9 %all_gather.11 = f32[4,4,6,512]{3,1,2,0:T(4,128)S(1)} all-gather(f32[1,4,6,512]{3,1,2,0:T(4,128)S(1)} %all_gather_reshape_reshape.3), channel_id=1, replica_groups=mesh['grp'=2,'gz'=4,'gx'=2,'row'=2] {'gx','row'}, dimensions={0}, use_global_device_ids=true | all-gather | bytes 245760 | tf_op jit(solution)/shard_map/all_gather | solution.py:119
  25.9 3.7 %collective-permute-start = (f32[4,2,512]{2,0,1:T(4,128)S(1)}, f32[4,2,512]{2,0,1:T(4,128)S(1)}, u32[]{:S(2)}, u32[]{:S(2)}) collective-permute-start(f32[4,2,512]{2,0,1:T(4,128)S(1)} %slice.82), channel_id=1, source_target_pairs={{0,4},{4,8},{8,12},{1,5},{5,9},{9,13},{2,6},{6,10},{10,14},{3,7},{... | collective-permute-start | bytes 49160 | tf_op jit(solution)/shard_map/ppermute | solution.py:16
  29.6 0.0 copy-done.4
  29.7 0.1 copy.98
  29.8 0.8 reshape.209
  30.6 3.9 %all-to-all-start = ((f32[1,4,768]{2,0,1:T(1,128)}), f32[1,4,768]{2,0,1:T(1,128)S(1)}, u32[]{:S(2)}, u32[]{:S(2)}) async-start(f32[1,4,768]{2,0,1:T(1,128)} %reshape.209), calls=%async_computation | async-start | bytes 24576 | tf_op jit(solution)/shard_map/all_to_all | solution.py:82
  34.5 0.0 copy-done.5
  34.5 0.3 copy.109
  34.8 0.2 copy.103
  35.0 0.8 reshape.210
  35.8 0.0 collective-permute-done
  35.8 1.3 %collective-permute-start.1 = (f32[4,2,512]{2,0,1:T(4,128)S(1)}, f32[4,2,512]{2,0,1:T(4,128)S(1)}, u32[]{:S(2)}, u32[]{:S(2)}) collective-permute-start(f32[4,2,512]{2,0,1:T(4,128)S(1)} %get-tuple-element.275), channel_id=1, source_target_pairs={{4,0},{8,4},{12,8},{5,1},{9,5},{13,9},{6,2},{10,6},{14,10},{7,3},{... | collective-permute-start | bytes 49160 | tf_op jit(solution)/shard_map/ppermute | solution.py:18
  37.1 3.0 %all-to-all-done = f32[1,4,768]{2,0,1:T(1,128)S(1)} async-done(((f32[1,4,768]{2,0,1:T(1,128)}), f32[1,4,768]{2,0,1:T(1,128)S(1)}, u32[]{:S(2)}, u32[]{:S(2)}) %all-to-all-start) | async-done | bytes 12320 | tf_op jit(solution)/shard_map/all_to_all | solution.py:82
  40.1 3.3 %all-to-all-start.1 = ((f32[1,4,768]{2,0,1:T(1,128)}), f32[1,4,768]{2,0,1:T(1,128)S(1)}, u32[]{:S(2)}, u32[]{:S(2)}) async-start(f32[1,4,768]{2,0,1:T(1,128)} %reshape.210), calls=%async_computation.1 | async-start | bytes 24576 | tf_op jit(solution)/shard_map/all_to_all | solution.py:81
  43.4 5.2 %all-gather = f32[1,4,3072]{2,0,1:T(1,128)S(1)} all-gather(f32[1,4,768]{2,0,1:T(1,128)S(1)} %all-to-all-done), channel_id=2, replica_groups=mesh['grp'=2,'gz'=4,'gx'=2,'row'=2] {'gx','row'}, dimensions={2}, use_global_device_ids=true | all-gather | bytes 61440 | tf_op jit(solution)/shard_map/all_gather | solution.py:88
  48.6 0.1 reduce.5
  48.7 1.0 %reshape.184 = f32[4,512,6]{2,1,0:T(8,128)S(1)} reshape(f32[4,3072]{1,0:T(4,128)S(1)} %reduce.5) | data formatting | bytes 98304 | tf_op jit(solution)/shard_map/reshape | solution.py:93
  49.7 0.3 copy.100
  50.1 0.0 all-to-all-done.1
  50.1 5.4 %all-gather.1 = f32[1,4,3072]{2,0,1:T(1,128)S(1)} all-gather(f32[1,4,768]{2,0,1:T(1,128)S(1)} %all-to-all-done.1), channel_id=3, replica_groups=mesh['grp'=2,'gz'=4,'gx'=2,'row'=2] {'gx','row'}, dimensions={2}, use_global_device_ids=true | all-gather | bytes 61440 | tf_op jit(solution)/shard_map/all_gather | solution.py:85
  55.5 0.1 reduce.6
  55.6 1.0 %reshape.189 = f32[4,512,6]{2,1,0:T(8,128)S(1)} reshape(f32[4,3072]{1,0:T(4,128)S(1)} %reduce.6) | data formatting | bytes 98304 | tf_op jit(solution)/shard_map/reshape | solution.py:92
  56.6 0.3 copy.105
  57.0 0.0 collective-permute-done.1
  57.0 24.8 %while.25 = (s32[]{:T(128)}, f32[2048,128]{1,0:T(8,128)}, s32[2,2,32,6,4]{2,3,4,1,0:T(8,128)S(1)}, s32[2,2]{1,0:T(2,128)S(1)}, bf16[2,2,6,4,128]{4,3,1,0,2:T(4,1...) while((s32[]{:T(128)}, f32[2048,128]{1,0:T(8,128)}, ...), condition=%wide.region_4.5_spmd.clone, body=%wide.region_3.4_spmd.clone.sunk | while | flops 1810370560 | bytes 12907599 | solution.py:150
  57.1 0.8 convert_bitcast_fusion.5
  57.9 0.7 fusion.113
  58.6 0.1 iota_compare_fusion.9
  58.7 4.7 %fusion.114 = f32[2048,128]{1,0:T(8,128)} fusion(s32[2,32,6,4]{1,2,3,0:T(8,128)S(1)} %dynamic-slice_bitcast_fusion.7, pred[2,32]{1,0:T(4,128)(4,1)S(1)} %iota_compare_fusion.9, f32[2,6,4,32,128]{4,1,3,2,0:T(8,128)S(1)} %fusion.113), kind=kOutput, calls=%fused_computation.36.clone.1 | convolution fusion | flops 811597824 | bytes 1841216 | tf_op jit(solution)/shard_map/while/body/eval_jaxpr/akwqn,akwqv->nv/dot_general | solution.py:139
  63.4 5.9 %fusion.115 = f32[2048,128]{1,0:T(8,128)} fusion(f32[2048,128]{1,0:T(8,128)} %fusion.114, s32[2,32,6,4]{1,2,3,0:T(8,128)S(1)} %dynamic-slice_bitcast_fusion.7, pred[2,32]{1,0:T(4,128)(4,1)S(1)} %iota_compare_fusion.9, f32[2048,128]{1,0:T(8,128)} %get-tuple-element.401, pred[]{:T(512)S(6)} %compare.16, f32[2,6,4,32,128]{4,1,3,2,0:T(8,128)S(1)} %fusion.113), kind=kOutput, calls=%fused_computation.39.clone.1 | convolution fusion | flops 813170688 | bytes 3938369 | tf_op jit(solution)/shard_map/while/body/eval_jaxpr/akwqn,akwqv->nv/dot_general | solution.py:142
  69.3 0.7 convert_bitcast_fusion.5
  70.1 0.7 fusion.113
  70.9 0.1 iota_compare_fusion.9
  70.9 4.7 %fusion.114 = f32[2048,128]{1,0:T(8,128)} fusion(s32[2,32,6,4]{1,2,3,0:T(8,128)S(1)} %dynamic-slice_bitcast_fusion.7, pred[2,32]{1,0:T(4,128)(4,1)S(1)} %iota_compare_fusion.9, f32[2,6,4,32,128]{4,1,3,2,0:T(8,128)S(1)} %fusion.113), kind=kOutput, calls=%fused_computation.36.clone.1 | convolution fusion | flops 811597824 | bytes 1841216 | tf_op jit(solution)/shard_map/while/body/eval_jaxpr/akwqn,akwqv->nv/dot_general | solution.py:139
  75.6 6.2 %fusion.115 = f32[2048,128]{1,0:T(8,128)} fusion(f32[2048,128]{1,0:T(8,128)} %fusion.114, s32[2,32,6,4]{1,2,3,0:T(8,128)S(1)} %dynamic-slice_bitcast_fusion.7, pred[2,32]{1,0:T(4,128)(4,1)S(1)} %iota_compare_fusion.9, f32[2048,128]{1,0:T(8,128)} %get-tuple-element.401, pred[]{:T(512)S(6)} %compare.16, f32[2,6,4,32,128]{4,1,3,2,0:T(8,128)S(1)} %fusion.113), kind=kOutput, calls=%fused_computation.39.clone.1 | convolution fusion | flops 813170688 | bytes 3938369 | tf_op jit(solution)/shard_map/while/body/eval_jaxpr/akwqn,akwqv->nv/dot_general | solution.py:142
  81.9 1.7 %reshape.193 = f32[4,256,256]{2,1,0:T(8,128)S(1)} reshape(f32[2048,128]{1,0:T(8,128)} %get-tuple-element.124) | data formatting | bytes 2097152 | tf_op jit(solution)/shard_map/reshape | solution.py:153
  83.6 0.0 copy-done
  83.6 0.2 copy-done.1
  83.7 1.2 %multiply_add_fusion = f32[4,256,256]{2,1,0:T(8,128)} fusion(f32[4,256,256]{2,1,0:T(8,128)S(1)} %copy-done, f32[4,256,256]{2,1,0:T(8,128)S(1)} %copy-done.1, f32[4,256,256]{2,1,0:T(8,128)S(1)} %reshape.193), kind=kLoop, calls=%fused_computation.60 | loop fusion | flops 524288 | bytes 4194304 | tf_op jit(solution)/shard_map/add | solution.py:153
  (37 shorter events, 0.4 us)
Async XLA Ops:
  0.0 3.0 %copy-start.3 = (s32[1,1,1,4,768]{4,3,2,1,0:T(4,128)S(1)}, s32[1,1,1,4,768]{4,3,2,1,0:T(4,128)}, u32[]{:S(2)}) copy-start(s32[1,1,1,4,768]{4,3,2,1,0:T(4,128)} %param.19) | copy-start | bytes 36868
  0.0 3.9 %copy-start.6 = (s32[1,1,1,4]{3,2,1,0:T(1,128)S(1)}, s32[1,1,1,4]{3,2,1,0:T(1,128)}, u32[]{:S(2)}) copy-start(s32[1,1,1,4]{3,2,1,0:T(1,128)} %param.20) | copy-start | bytes 52
  3.0 4.0 %copy-start.2 = (s32[1,1,1,4,32]{4,3,2,1,0:T(4,128)S(1)}, s32[1,1,1,4,32]{4,3,2,1,0:T(4,128)}, u32[]{:S(2)}) copy-start(s32[1,1,1,4,32]{4,3,2,1,0:T(4,128)} %param.18) | copy-start | bytes 1540
  6.9 22.7 %copy-start.4 = (f32[1,128,16]{1,2,0:T(8,128)S(1)}, f32[1,128,16]{1,2,0:T(8,128)}, u32[]{:S(2)}) copy-start(f32[1,128,16]{1,2,0:T(8,128)} %param.22) | copy-start | bytes 24580
  6.9 27.5 %copy-start.5 = (f32[1,128,16]{1,2,0:T(8,128)S(1)}, f32[1,128,16]{1,2,0:T(8,128)}, u32[]{:S(2)}) copy-start(f32[1,128,16]{1,2,0:T(8,128)} %param.21) | copy-start | bytes 24580
  25.9 9.9 %collective-permute-start = (f32[4,2,512]{2,0,1:T(4,128)S(1)}, f32[4,2,512]{2,0,1:T(4,128)S(1)}, u32[]{:S(2)}, u32[]{:S(2)}) collective-permute-start(f32[4,2,512]{2,0,1:T(4,128)S(1)} %slice.82), channel_id=1, source_target_pairs={{0,4},{4,8},{8,12},{1,5},{5,9},{9,13},{2,6},{6,10},{10,14},{3,7},{... | collective-permute-start | bytes 49160 | tf_op jit(solution)/shard_map/ppermute | solution.py:16
  30.6 9.5 %all-to-all-start = ((f32[1,4,768]{2,0,1:T(1,128)}), f32[1,4,768]{2,0,1:T(1,128)S(1)}, u32[]{:S(2)}, u32[]{:S(2)}) async-start(f32[1,4,768]{2,0,1:T(1,128)} %reshape.209), calls=%async_computation | async-start | bytes 24576 | tf_op jit(solution)/shard_map/all_to_all | solution.py:82
  35.8 21.2 %collective-permute-start.1 = (f32[4,2,512]{2,0,1:T(4,128)S(1)}, f32[4,2,512]{2,0,1:T(4,128)S(1)}, u32[]{:S(2)}, u32[]{:S(2)}) collective-permute-start(f32[4,2,512]{2,0,1:T(4,128)S(1)} %get-tuple-element.275), channel_id=1, source_target_pairs={{4,0},{8,4},{12,8},{5,1},{9,5},{13,9},{6,2},{10,6},{14,10},{7,3},{... | collective-permute-start | bytes 49160 | tf_op jit(solution)/shard_map/ppermute | solution.py:18
  40.1 10.0 %all-to-all-start.1 = ((f32[1,4,768]{2,0,1:T(1,128)}), f32[1,4,768]{2,0,1:T(1,128)S(1)}, u32[]{:S(2)}, u32[]{:S(2)}) async-start(f32[1,4,768]{2,0,1:T(1,128)} %reshape.210), calls=%async_computation.1 | async-start | bytes 24576 | tf_op jit(solution)/shard_map/all_to_all | solution.py:81
  81.9 1.7 %copy-start = (f32[4,256,256]{2,1,0:T(8,128)S(1)}, f32[4,256,256]{2,1,0:T(8,128)}, u32[]{:S(2)}) copy-start(f32[4,256,256]{2,1,0:T(8,128)} %param.16) | copy-start | bytes 3145732
  81.9 1.9 %copy-start.1 = (f32[4,256,256]{2,1,0:T(8,128)S(1)}, f32[4,256,256]{2,1,0:T(8,128)}, u32[]{:S(2)}) copy-start(f32[4,256,256]{2,1,0:T(8,128)} %param.23) | copy-start | bytes 3145732
